TPU v7x, 128 devices: a whole 4x4x4 slice. The times are simulated.
128 devices in a mesh: slab: 16 (over y, x), lev: 8 (over z, core).
Axes of the slice: x: 4, y: 4, z: 4, core: 2. Of those that a mesh axis runs over, the one named last changes fastest.
Arguments:
- ensemble: float32 [80, 32, 36864], P(None, 'lev', 'slab'), may hold values from -6 to 6
- obs_cell: int32 [2, 256], replicated, may hold values from 0 to 1179647, as said below
- obs_value: float32 [2, 256], replicated, may hold values from -6 to 6
- obs_var: float32 [2, 256], replicated, may hold values from 0.3 to 3
- obs_frac: float32 [2, 256], replicated, may hold values from 0 to 1
- loc_column: bfloat16 [2, 256, 36864], P(None, 'lev', 'slab'), may hold values from 0 to 1
- loc_level: float32 [2, 256, 32], P(None, None, 'lev'), may hold values from 0.2 to 1
Outputs:
- analysis: float32 [80, 32, 36864], P(None, 'lev', 'slab')
- prior_mean: float32 [2, 256], replicated
Inputs may be any that keep to these rules, and one draw needn't show every extreme that they name: `obs_cell`: in each block, every device's cells (a level band of 4 levels and a slab of 2304 columns) hold at least one observation, and one of them lies in the slab's last column.
All inputs are finite; a program needn't handle non-finite values.
Results may differ from a plain program's by a relative error of at most 0.0055.
Values may be sent and summed in bfloat16 or wider, within the bound.
A program may use at most 64 MiB of HBM per device.

v0:
```python
import jax
import jax.numpy as jnp
from jax import lax
from jax.sharding import PartitionSpec as P


def laid_out(parts, dim):
    parts = jnp.moveaxis(parts, 0, dim)
    shape = parts.shape
    return parts.reshape(*shape[:dim], shape[dim] * shape[dim + 1], *shape[dim + 2 :])


def sent_to_all(array, axis):
    copies = jnp.broadcast_to(array, (lax.axis_size(axis), *array.shape))
    return lax.all_to_all(copies, axis, split_axis=0, concat_axis=0, tiled=True)


def gather_directly(array, axis, dim):
    return laid_out(sent_to_all(array, axis), dim)


def obs_stats(prior_obs, obs_val, variance):
    members = prior_obs.shape[1]
    obs_mean = jnp.mean(prior_obs, axis=1)
    deviation = prior_obs - obs_mean[:, None]
    spread = jnp.sum(deviation * deviation, axis=1) / (members - 1.0)
    total_var = spread + variance
    shrink = 1.0 / (1.0 + jnp.sqrt(variance / total_var))
    gain_rows = ((obs_val - obs_mean)[:, None] - deviation * shrink[:, None]) / (
        total_var * (members - 1.0)
    )[:, None]
    return (obs_mean, deviation.astype(jnp.bfloat16), gain_rows.astype(jnp.bfloat16))


def cell_values(current, levels, columns):
    members, lev_rows, slab_cols = current.shape
    local_row = levels - lax.axis_index("lev") * lev_rows
    local_col = columns - lax.axis_index("slab") * slab_cols
    inside = (local_row >= 0) & (local_row < lev_rows) & (local_col >= 0) & (local_col < slab_cols)
    row_safe = jnp.clip(local_row, 0, lev_rows - 1)
    col_safe = jnp.clip(local_col, 0, slab_cols - 1)
    flattened = current.reshape(members, lev_rows * slab_cols)
    picked = jnp.take(flattened, row_safe * slab_cols + col_safe, axis=1)
    return jnp.where(inside[None, :], picked, 0.0).T


def column_table(loc_block, columns):
    rows_local, slab_cols = loc_block.shape
    local_col = columns - lax.axis_index("slab") * slab_cols
    inside = (local_col >= 0) & (local_col < slab_cols)
    col_safe = jnp.clip(local_col, 0, slab_cols - 1)
    picked = jnp.take(loc_block, col_safe, axis=1).astype(jnp.float32)
    picked = jnp.where(inside[None, :], picked, 0.0)
    holder = jnp.zeros((rows_local * lax.axis_size("lev"), columns.shape[0]), jnp.float32)
    return lax.dynamic_update_slice(
        holder, picked, (lax.axis_index("lev") * rows_local, jnp.int32(0))
    )


def level_table(lev_block, levels):
    lev_rows = lev_block.shape[1]
    local_row = levels - lax.axis_index("lev") * lev_rows
    inside = (local_row >= 0) & (local_row < lev_rows) & (lax.axis_index("slab") == 0)
    row_safe = jnp.clip(local_row, 0, lev_rows - 1)
    picked = jnp.take(lev_block, row_safe, axis=1)
    return jnp.where(inside[None, :], picked, 0.0)


def cell_update(values, dev_b, gain_b, col_table, lev_table):
    centred_cells = (values - jnp.mean(values, axis=1)[:, None]).astype(jnp.bfloat16)
    cross_cov = jnp.dot(dev_b, centred_cells.T, preferred_element_type=jnp.float32)
    mixed_rows = (lev_table * col_table * cross_cov).astype(jnp.bfloat16)
    return values + jnp.dot(gain_b.T, mixed_rows, preferred_element_type=jnp.float32).T


def regress_rows(running, loc_piece, row_start, centred, dev_b, gain_b, lev_weights):
    row_total = loc_piece.shape[0]
    row_step = min(row_total, 64)
    lev_rows = lev_weights.shape[1]
    slab_cols = loc_piece.shape[1]
    for offset in range(0, row_total, row_step):
        row_count = min(row_step, row_total - offset)
        row_piece = loc_piece[offset : offset + row_count]
        dev_rows = lax.dynamic_slice_in_dim(dev_b, row_start + offset, row_count, 0)
        gain_rows = lax.dynamic_slice_in_dim(gain_b, row_start + offset, row_count, 0)
        level_loc = lax.dynamic_slice_in_dim(lev_weights, row_start + offset, row_count, 0)
        cross_cov = jnp.dot(dev_rows, centred, preferred_element_type=jnp.float32).reshape(
            row_count, lev_rows, slab_cols
        )
        weights = level_loc[:, :, None] * row_piece[:, None, :].astype(jnp.float32)
        mixed_rows = (
            (weights * cross_cov).astype(jnp.bfloat16).reshape(row_count, lev_rows * slab_cols)
        )
        running = running + jnp.dot(gain_rows.T, mixed_rows, preferred_element_type=jnp.float32)
    return running


def on_device(ensemble, obs_cell, obs_value, obs_var, obs_frac, loc_column, loc_level):
    members, lev_rows, slab_cols = ensemble.shape
    n_blocks = obs_cell.shape[0]
    total_cols = slab_cols * lax.axis_size("slab")
    pair_index = {}
    pieces = []
    for later in range(n_blocks):
        levels = obs_cell[later] // total_cols
        columns = obs_cell[later] % total_cols
        next_cols = (columns + 1) % total_cols
        pieces.append(cell_values(ensemble, levels, columns))
        pieces.append(cell_values(ensemble, levels, next_cols))
        for earlier in range(later):
            pair_index[earlier, later] = len(pieces)
            pieces.append(column_table(loc_column[earlier], columns))
            pieces.append(column_table(loc_column[earlier], next_cols))
            pieces.append(level_table(loc_level[earlier], levels))
    summed = lax.psum(tuple(pieces), ("slab", "lev"))
    raw_first = []
    raw_second = []
    position = 0
    for later in range(n_blocks):
        raw_first.append(summed[position])
        raw_second.append(summed[position + 1])
        position = position + 2 + 3 * later
    columns_all = gather_directly(loc_column, "lev", 1)
    current = ensemble
    prior_means = []
    for block_index in range(n_blocks):
        fraction = obs_frac[block_index]
        prior_obs = (1.0 - fraction)[:, None] * raw_first[block_index] + fraction[
            :, None
        ] * raw_second[block_index]
        obs_mean, dev_b, gain_b = obs_stats(prior_obs, obs_value[block_index], obs_var[block_index])
        prior_means.append(obs_mean)
        centred = (
            (current - jnp.mean(current, axis=0))
            .astype(jnp.bfloat16)
            .reshape(members, lev_rows * slab_cols)
        )
        lev_weights = loc_level[block_index]
        zero_incr = jnp.zeros((members, lev_rows * slab_cols), jnp.float32)
        increment = regress_rows(
            zero_incr, columns_all[block_index], 0, centred, dev_b, gain_b, lev_weights
        )
        for later in range(block_index + 1, n_blocks):
            start_at = pair_index[block_index, later]
            col_first = summed[start_at]
            col_second = summed[start_at + 1]
            lev_table = summed[start_at + 2]
            raw_first[later] = cell_update(raw_first[later], dev_b, gain_b, col_first, lev_table)
            raw_second[later] = cell_update(raw_second[later], dev_b, gain_b, col_second, lev_table)
        current = current + increment.reshape(members, lev_rows, slab_cols)
    return (current, jnp.stack(prior_means))


def solution(mesh):
    in_specs = (
        P(None, "lev", "slab"),
        P(),
        P(),
        P(),
        P(),
        P(None, "lev", "slab"),
        P(None, None, "lev"),
    )
    out_specs = (P(None, "lev", "slab"), P())
    return jax.shard_map(
        on_device, mesh=mesh, in_specs=in_specs, out_specs=out_specs, check_vma=False
    )
```

profile of v0, /device:TPU:1, one launch (start us, length us, event | category | flops | bytes accessed | tf_op | source)
XLA Modules:
  0.0 267.5 jit_solution(16684422704884585923)
XLA Ops:
  7.2 2.6 broadcast_in_dim.147
  9.8 7.1 %all-to-all-start = ((bf16[8,2,32,2304]{3,2,1,0:T(8,128)(2,1)}), bf16[8,2,32,2304]{3,2,1,0:T(8,128)(2,1)}, u32[]{:S(2)}, u32[]{:S(2)}) async-start(bf16[8,2,32,2304]{3,2,1,0:T(8,128)(2,1)} %broadcast_in_dim.147), calls=%async_computation | async-start | bytes 4718592 | tf_op jit(solution)/shard_map/all_to_all | solution.py:15
  16.9 0.7 slice.107
  17.6 3.5 %copy.35 = f32[80,4,2304]{0,2,1:T(8,128)} copy(f32[80,4,2304]{2,1,0:T(4,128)S(1)} %copy-done) | data formatting | bytes 5898240 | tf_op args[0]
  21.1 0.6 fusion.72
  21.7 1.1 and_reduce_fusion.6
  22.8 0.6 compare_and_fusion.3
  23.4 3.7 %gather_fusion.2 = f32[256,80]{1,0:T(8,128)} fusion(f32[80,9216]{0,1:T(8,128)} %bitcast.212, s32[1024]{0:T(1024)S(1)} %pad_clamp_fusion.5), kind=kCustom, calls=%fused_computation.2.clone | custom fusion | bytes 164864 | tf_op jit(solution)/shard_map/jit(_take)/gather | solution.py:43
  27.1 3.7 %gather_fusion.1 = f32[256,80]{1,0:T(8,128)} fusion(f32[80,9216]{0,1:T(8,128)} %bitcast.213, s32[1024]{0:T(1024)S(1)} %pad_clamp_fusion.6), kind=kCustom, calls=%fused_computation.clone | custom fusion | bytes 164864 | tf_op jit(solution)/shard_map/jit(_take)/gather | solution.py:43
  30.8 0.6 compare_select_fusion.1
  31.4 0.6 compare_and_fusion.5
  32.5 3.7 %gather_fusion.3 = f32[256,80]{1,0:T(8,128)} fusion(f32[80,9216]{0,1:T(8,128)} %bitcast.214, s32[1024]{0:T(1024)S(1)} %pad_clamp_fusion.4), kind=kCustom, calls=%fused_computation.3.clone | custom fusion | bytes 164864 | tf_op jit(solution)/shard_map/jit(_take)/gather | solution.py:43
  36.2 1.0 gather_fusion
  37.1 0.9 copy.44
  38.0 1.2 copy.61
  39.3 1.5 gather_fusion.4
  40.7 0.9 copy.47
  41.6 1.3 pad_clamp_fusion.1
  42.9 3.8 %gather_fusion.5 = f32[256,80]{1,0:T(8,128)} fusion(f32[80,9216]{0,1:T(8,128)} %bitcast.215, s32[1024]{0:T(1024)} %pad_clamp_fusion.1), kind=kCustom, calls=%fused_computation.4.clone | custom fusion | bytes 164864 | tf_op jit(solution)/shard_map/jit(_take)/gather | solution.py:43
  46.7 1.2 pad_clamp_fusion
  48.0 1.6 gather_fusion.6
  49.6 0.9 copy.49
  50.5 1.7 fusion.45
  52.2 1.7 fusion.46
  53.9 0.7 and_reduce_fusion
  54.7 1.7 fusion.44
  56.4 1.7 select_bitcast_fusion
  58.1 1.5 fusion.43
  59.7 0.6 copy-done.12
  60.4 0.7 slice_bitcast_fusion.17
  61.7 1.7 subtract_convert_fusion.1
  63.4 150.0 %all-reduce.3.cloned.1.call-done = (f32[256,80]{1,0:T(8,128)}, f32[256,80]{1,0:T(8,128)}, f32[256,80]{1,0:T(8,128)}, f32[256,256]{1,0:T(8,128)}, f32[256,256]{1,...) async-done(((f32[256,80]{1,0:T(8,128)}, f32[256,80]{1,0:T(8,128)}, f32[256,80]{1,0:T(8,128)}, f32[256,256]{1,0:T(8,128)}, f32[256,256]{1,0:T(8,128)}, ...) | async-done | bytes 1114128 | tf_op jit(solution)/shard_map/psum | solution.py:115
  213.3 1.0 reduce_sum.75
  214.4 1.2 fusion.80
  215.8 1.0 reduce_sum.76
  217.1 2.3 fusion.32
  219.4 1.7 fusion.87
  221.1 0.6 pad_maximum_fusion
  221.9 0.9 divide_convert_fusion
  222.8 2.6 fusion.83
  225.5 1.2 copy-done.1
  226.8 0.6 fusion.15
  227.4 0.7 copy-done.7
  228.2 0.6 fusion.59
  230.2 0.6 fusion.13
  230.8 0.6 copy-done.20
  231.4 0.6 fusion.12
  232.1 0.6 convolution_add_fusion.5
  232.6 0.6 convolution_add_fusion.4
  233.2 2.2 convolution_add_fusion.3
  235.4 4.5 %reshape.387 = f32[80,4,2304]{2,1,0:T(4,128)} reshape(f32[80,9216]{1,0:T(8,128)} %convolution_add_fusion.3) | data formatting | bytes 5898240 | tf_op jit(solution)/shard_map/reshape | solution.py:150
  239.9 2.8 %fusion.79 = (f32[4,2304]{1,0:T(4,128)S(1)}, f32[80,4,2304]{2,1,0:T(4,128)S(1)}) fusion(f32[80,4,2304]{2,1,0:T(4,128)S(1)} %copy-done, f32[80,4,2304]{2,1,0:T(4,128)} %reshape.387), kind=kLoop, calls=%fused_computation.210 | loop fusion | flops 1465344 | bytes 8884224 | tf_op jit(solution)/shard_map/reduce_sum | solution.py:134
  243.4 0.9 copy-done.2
  244.3 0.6 fusion.11
  245.0 0.6 fusion.10
  245.8 0.6 fusion.9
  246.4 0.6 fusion.8
  247.1 0.7 copy-done.15
  247.8 0.6 fusion.54
  248.4 0.6 convolution_add_fusion.2
  249.0 0.6 convolution_add_fusion.1
  249.6 2.2 convolution_add_fusion
  251.8 4.7 %reshape.393 = f32[80,4,2304]{2,1,0:T(4,128)} reshape(f32[80,9216]{1,0:T(8,128)} %convolution_add_fusion) | data formatting | bytes 5898240 | tf_op jit(solution)/shard_map/reshape | solution.py:150
  256.4 4.2 %add.227 = f32[80,4,2304]{2,1,0:T(4,128)} add(f32[80,4,2304]{2,1,0:T(4,128)S(1)} %copy-done.3, f32[80,4,2304]{2,1,0:T(4,128)} %reshape.393) | non-fusion elementwise | flops 737280 | bytes 8847360 | tf_op jit(solution)/shard_map/add | solution.py:150
  (99 shorter events, 4.9 us)
Async XLA Ops:
  9.8 7.1 %copy-start.19 = (s32[2,256]{1,0:T(2,128)S(1)}, s32[2,256]{1,0:T(2,128)}, u32[]{:S(2)}) copy-start(s32[2,256]{1,0:T(2,128)} %param.12) | copy-start | bytes 6148
  9.8 7.1 %copy-start.13 = (bf16[2,32,2304]{2,1,0:T(8,128)(2,1)S(1)}, bf16[2,32,2304]{2,1,0:T(8,128)(2,1)}, u32[]{:S(2)}) copy-start(bf16[2,32,2304]{2,1,0:T(8,128)(2,1)} %param.16) | copy-start | bytes 884740
  9.8 7.8 %copy-start = (f32[80,4,2304]{2,1,0:T(4,128)S(1)}, f32[80,4,2304]{2,1,0:T(4,128)}, u32[]{:S(2)}) copy-start(f32[80,4,2304]{2,1,0:T(4,128)} %param.11) | copy-start | bytes 8847364
  9.8 213.0 %all-to-all-start = ((bf16[8,2,32,2304]{3,2,1,0:T(8,128)(2,1)}), bf16[8,2,32,2304]{3,2,1,0:T(8,128)(2,1)}, u32[]{:S(2)}, u32[]{:S(2)}) async-start(bf16[8,2,32,2304]{3,2,1,0:T(8,128)(2,1)} %broadcast_in_dim.147), calls=%async_computation | async-start | bytes 4718592 | tf_op jit(solution)/shard_map/all_to_all | solution.py:15
  16.8 196.5 %all-reduce.3.cloned.1.call-start = ((), (), s32[]{:S(2)}) async-start(), calls=%async_computation.1 | async-start | bytes 2621440 | tf_op jit(solution)/shard_map/psum | solution.py:115
  21.1 15.1 %copy-start.17 = (f32[2,256,4]{1,2,0:T(4,128)S(1)}, f32[2,256,4]{1,2,0:T(4,128)}, u32[]{:S(2)}) copy-start(f32[2,256,4]{1,2,0:T(4,128)} %param.17) | copy-start | bytes 24580
  49.6 8.5 %copy-start.14 = (f32[256,80]{1,0:T(8,128)S(1)}, f32[256,80]{1,0:T(8,128)}, u32[]{:S(2)}) copy-start(f32[256,80]{1,0:T(8,128)} %gather_fusion.5) | copy-start | bytes 245764
  49.6 10.0 %copy-start.25 = (pred[256]{0:T(512)(128)(4,1)S(1)}, pred[256]{0:T(512)(128)(4,1)}, u32[]{:S(2)}) copy-start(pred[256]{0:T(512)(128)(4,1)} %get-tuple-element.29) | copy-start | bytes 772
  49.6 10.1 %copy-start.24 = (pred[256]{0:T(512)(128)(4,1)S(1)}, pred[256]{0:T(512)(128)(4,1)}, u32[]{:S(2)}) copy-start(pred[256]{0:T(512)(128)(4,1)} %get-tuple-element.24) | copy-start | bytes 772
  54.6 5.8 %copy-start.18 = (f32[2,256,4]{1,2,0:T(4,128)S(1)}, f32[2,256,4]{1,2,0:T(4,128)}, u32[]{:S(2)}) copy-start(f32[2,256,4]{1,2,0:T(4,128)} %param.17) | copy-start | bytes 24580
  54.7 6.4 %copy-start.26 = (f32[2,256]{1,0:T(2,128)S(1)}, f32[2,256]{1,0:T(2,128)}, u32[]{:S(2)}) copy-start(f32[2,256]{1,0:T(2,128)} %param.15) | copy-start | bytes 6148
  54.7 6.5 %copy-start.27 = (f32[2,256]{1,0:T(2,128)S(1)}, f32[2,256]{1,0:T(2,128)}, u32[]{:S(2)}) copy-start(f32[2,256]{1,0:T(2,128)} %param.14) | copy-start | bytes 6148
  54.7 6.5 %copy-start.28 = (f32[2,256]{1,0:T(2,128)S(1)}, f32[2,256]{1,0:T(2,128)}, u32[]{:S(2)}) copy-start(f32[2,256]{1,0:T(2,128)} %param.13) | copy-start | bytes 6148
  59.6 0.7 copy-start.12
  59.7 0.7 copy-start.11
  213.3 6.1 %copy-start.10 = (f32[256,256]{1,0:T(8,128)S(1)}, f32[256,256]{1,0:T(8,128)}, u32[]{:S(2)}) copy-start(f32[256,256]{1,0:T(8,128)} %get-tuple-element.16) | copy-start | bytes 786436
  217.0 5.7 %copy-start.6 = (bf16[256,80]{1,0:T(8,128)(2,1)}, bf16[256,80]{1,0:T(8,128)(2,1)S(1)}, u32[]{:S(2)}) copy-start(bf16[256,80]{1,0:T(8,128)(2,1)S(1)} %get-tuple-element.53) | copy-start | bytes 122884
  217.1 5.7 %copy-start.8 = (bf16[256,80]{1,0:T(8,128)(2,1)}, bf16[256,80]{1,0:T(8,128)(2,1)S(1)}, u32[]{:S(2)}) copy-start(bf16[256,80]{1,0:T(8,128)(2,1)S(1)} %get-tuple-element.54) | copy-start | bytes 122884
  225.4 1.4 copy-start.1
  225.4 1.4 copy-start.9
  225.4 1.4 copy-start.23
  227.3 0.8 copy-start.7
  228.2 0.7 copy-start.22
  229.5 0.7 copy-start.21
  230.7 0.7 copy-start.20
  239.9 2.9 %copy-start.4 = (bf16[1,2,32,2304]{3,2,0,1:T(8,128)(2,1)S(1)}, bf16[1,2,32,2304]{3,2,0,1:T(8,128)(2,1)}, u32[]{:S(2)}) copy-start(bf16[1,2,32,2304]{3,2,0,1:T(8,128)(2,1)} %get-tuple-element.45) | copy-start | bytes 884740
  239.9 2.9 %copy-start.5 = (bf16[1,2,32,2304]{3,2,0,1:T(8,128)(2,1)S(1)}, bf16[1,2,32,2304]{3,2,0,1:T(8,128)(2,1)}, u32[]{:S(2)}) copy-start(bf16[1,2,32,2304]{3,2,0,1:T(8,128)(2,1)} %get-tuple-element.46) | copy-start | bytes 884740
  242.7 1.6 copy-start.2
  242.9 1.4 copy-start.16
  247.0 0.8 copy-start.15
  251.7 4.7 %copy-start.3 = (f32[80,4,2304]{2,1,0:T(4,128)S(1)}, f32[80,4,2304]{2,1,0:T(4,128)}, u32[]{:S(2)}) copy-start(f32[80,4,2304]{2,1,0:T(4,128)} %copy-done.2) | copy-start | bytes 8847364
Sparse Core Ops, SparseCore 0:
  60.5 152.7 all-reduce.2
where the time goes:
time: 269 us; the launch traced here: 267 us
  waiting for transfers between devices  150 us (56%)
  local copies, waits for them, and re-layouts  48.4 us (18%)
  other arithmetic  31.1 us (12%)
  matrix products  16.3 us (6%)
  between operations  14.6 us (5%)
  starting transfers between devices  7.07 us (3%)
    psum x1, waiting for transfers between devices, on_device(): summed = lax.psum(tuple(pieces), ('slab', 'lev'))  150 us
    gather x4, local copies, waits for them, and re-layouts, cell_values(): picked = jnp.take(flattened, row_safe * slab_cols + col_safe, axis=1)  14.8 us
    unnamed x60, local copies, waits for them, and re-layouts  10.4 us
    reshape x2, local copies, waits for them, and re-layouts, on_device(): current = current + increment.reshape(members, lev_rows, slab_cols)  9.15 us
    dot_general x8, matrix products, regress_rows(): jnp.dot(gain_rows.T, mixed_rows, preferred_element_type=jnp.float32)  7.74 us
    all_to_all x1, starting transfers between devices, sent_to_all(): return lax.all_to_all(copies, axis, split_axis=0, concat_axis=0, tiled=True)  7.07 us
    transpose x4, other arithmetic, cell_values(): return jnp.where(inside[None, :], picked, 0.0).T  6.56 us
  transfers between devices with their start and end apart: 2, of which 1 were waited for; matrix products, arithmetic and copies ran while one was open for 21% of the time, Pallas kernels for 0%

commit v1 on v0

--- a/solution.py
+++ b/solution.py
@@ -112,7 +112,8 @@
             pieces.append(column_table(loc_column[earlier], columns))
             pieces.append(column_table(loc_column[earlier], next_cols))
             pieces.append(level_table(loc_level[earlier], levels))
-    summed = lax.psum(tuple(pieces), ("slab", "lev"))
+    half = lax.psum(tuple(pieces), "slab")
+    summed = lax.psum(half, "lev")
     raw_first = []
     raw_second = []
     position = 0

time: 269 us -> 272 us (1.011)
  waiting for transfers between devices: 150 us -> 153 us
    psum x1 -> x2, waiting for transfers between devices: 150 us -> 153 us  [the longest x1 87.5 us: on_device(): half = lax.psum(tuple(pieces), 'slab')]
  transfers between devices with their start and end apart: 2 -> 3, of which waited for: 1 -> 2; matrix products, arithmetic and copies ran while one was open for 21% -> 20% of each run, Pallas kernels for 0% -> 0%
where the time goes in v1:
time: 272 us; the launch traced here: 270 us
  waiting for transfers between devices  153 us (56%)
  local copies, waits for them, and re-layouts  48.5 us (18%)
  other arithmetic  31 us (11%)
  matrix products  16.3 us (6%)
  between operations  14.6 us (5%)
  starting transfers between devices  7.11 us (3%)
    psum x1, waiting for transfers between devices, on_device(): half = lax.psum(tuple(pieces), 'slab')  87.5 us
    psum x1, waiting for transfers between devices, on_device(): summed = lax.psum(half, 'lev')  65.1 us
    gather x4, local copies, waits for them, and re-layouts, cell_values(): picked = jnp.take(flattened, row_safe * slab_cols + col_safe, axis=1)  14.8 us
    unnamed x60, local copies, waits for them, and re-layouts  10.6 us
    reshape x2, local copies, waits for them, and re-layouts, on_device(): current = current + increment.reshape(members, lev_rows, slab_cols)  9.17 us
    dot_general x8, matrix products, regress_rows(): jnp.dot(gain_rows.T, mixed_rows, preferred_element_type=jnp.float32)  7.77 us
    all_to_all x1, starting transfers between devices, sent_to_all(): return lax.all_to_all(copies, axis, split_axis=0, concat_axis=0, tiled=True)  7.07 us
    transpose x4, other arithmetic, cell_values(): return jnp.where(inside[None, :], picked, 0.0).T  6.57 us
  transfers between devices with their start and end apart: 3, of which 2 were waited for; matrix products, arithmetic and copies ran while one was open for 20% of the time, Pallas kernels for 0%

profile of v1, /device:TPU:1, one launch (start us, length us, event | category | flops | bytes accessed | tf_op | source)
XLA Modules:
  0.0 270.2 jit_solution(5789260087251405276)
XLA Ops:
  7.2 2.6 broadcast_in_dim.147
  9.8 7.1 %all-to-all-start = ((bf16[8,2,32,2304]{3,2,1,0:T(8,128)(2,1)}), bf16[8,2,32,2304]{3,2,1,0:T(8,128)(2,1)}, u32[]{:S(2)}, u32[]{:S(2)}) async-start(bf16[8,2,32,2304]{3,2,1,0:T(8,128)(2,1)} %broadcast_in_dim.147), calls=%async_computation | async-start | bytes 4718592 | tf_op jit(solution)/shard_map/all_to_all | solution.py:15
  16.9 0.7 slice.107
  17.6 3.6 %copy.35 = f32[80,4,2304]{0,2,1:T(8,128)} copy(f32[80,4,2304]{2,1,0:T(4,128)S(1)} %copy-done) | data formatting | bytes 5898240 | tf_op args[0]
  21.1 0.6 fusion.72
  21.7 1.1 and_reduce_fusion.6
  22.8 0.6 compare_and_fusion.3
  23.4 3.7 %gather_fusion.2 = f32[256,80]{1,0:T(8,128)} fusion(f32[80,9216]{0,1:T(8,128)} %bitcast.212, s32[1024]{0:T(1024)S(1)} %pad_clamp_fusion.5), kind=kCustom, calls=%fused_computation.2.clone | custom fusion | bytes 164864 | tf_op jit(solution)/shard_map/jit(_take)/gather | solution.py:43
  27.1 3.7 %gather_fusion.1 = f32[256,80]{1,0:T(8,128)} fusion(f32[80,9216]{0,1:T(8,128)} %bitcast.213, s32[1024]{0:T(1024)S(1)} %pad_clamp_fusion.6), kind=kCustom, calls=%fused_computation.clone | custom fusion | bytes 164864 | tf_op jit(solution)/shard_map/jit(_take)/gather | solution.py:43
  31.3 0.6 compare_and_fusion.5
  32.5 3.7 %gather_fusion.3 = f32[256,80]{1,0:T(8,128)} fusion(f32[80,9216]{0,1:T(8,128)} %bitcast.214, s32[1024]{0:T(1024)S(1)} %pad_clamp_fusion.4), kind=kCustom, calls=%fused_computation.3.clone | custom fusion | bytes 164864 | tf_op jit(solution)/shard_map/jit(_take)/gather | solution.py:43
  36.2 1.0 gather_fusion
  37.1 0.8 copy.44
  38.0 1.2 copy.61
  39.2 1.5 gather_fusion.4
  40.7 0.9 copy.47
  41.6 1.2 pad_clamp_fusion.1
  42.8 3.8 %gather_fusion.5 = f32[256,80]{1,0:T(8,128)} fusion(f32[80,9216]{0,1:T(8,128)} %bitcast.215, s32[1024]{0:T(1024)} %pad_clamp_fusion.1), kind=kCustom, calls=%fused_computation.4.clone | custom fusion | bytes 164864 | tf_op jit(solution)/shard_map/jit(_take)/gather | solution.py:43
  46.6 1.2 pad_clamp_fusion
  47.8 1.6 gather_fusion.6
  49.4 0.9 copy.49
  50.4 1.7 fusion.45
  52.1 1.7 fusion.46
  53.8 0.7 and_reduce_fusion
  54.5 1.7 fusion.44
  56.2 1.7 select_bitcast_fusion
  57.9 1.5 fusion.43
  59.5 0.6 copy-done.12
  61.1 0.6 slice_bitcast_fusion.17
  61.7 87.5 %all-reduce.5.cloned.1.call-done = (f32[256,80]{1,0:T(8,128)}, f32[256,80]{1,0:T(8,128)}, f32[256,80]{1,0:T(8,128)}, f32[256,256]{1,0:T(8,128)}, f32[256,256]{1,...) async-done(((f32[256,80]{1,0:T(8,128)}, f32[256,80]{1,0:T(8,128)}, f32[256,80]{1,0:T(8,128)}, f32[256,256]{1,0:T(8,128)}, f32[256,256]{1,0:T(8,128)}, ...) | async-done | bytes 1114128 | tf_op jit(solution)/shard_map/psum | solution.py:115
  149.3 1.6 subtract_convert_fusion.1
  150.9 65.1 %all-reduce.7.cloned.1.call-done = (f32[256,80]{1,0:T(8,128)}, f32[256,80]{1,0:T(8,128)}, f32[256,80]{1,0:T(8,128)}, f32[256,256]{1,0:T(8,128)}, f32[256,256]{1,...) async-done(((f32[256,80]{1,0:T(8,128)}, f32[256,80]{1,0:T(8,128)}, f32[256,80]{1,0:T(8,128)}, f32[256,256]{1,0:T(8,128)}, f32[256,256]{1,0:T(8,128)}, ...) | async-done | bytes 1114128 | tf_op jit(solution)/shard_map/psum | solution.py:116
  216.1 1.0 reduce_sum.75
  217.1 1.2 fusion.80
  218.5 1.0 reduce_sum.76
  219.8 2.3 fusion.32
  222.1 1.7 fusion.87
  223.8 0.6 pad_maximum_fusion
  224.6 0.9 divide_convert_fusion
  225.5 2.6 fusion.83
  228.2 1.2 copy-done.1
  229.5 0.6 fusion.15
  230.1 0.7 copy-done.7
  230.9 0.6 fusion.59
  231.5 0.6 fusion.14
  232.9 0.6 fusion.13
  233.5 0.6 copy-done.20
  234.7 0.6 convolution_add_fusion.5
  235.3 0.6 convolution_add_fusion.4
  235.9 2.2 convolution_add_fusion.3
  238.1 4.5 %reshape.387 = f32[80,4,2304]{2,1,0:T(4,128)} reshape(f32[80,9216]{1,0:T(8,128)} %convolution_add_fusion.3) | data formatting | bytes 5898240 | tf_op jit(solution)/shard_map/reshape | solution.py:151
  242.6 2.8 %fusion.79 = (f32[4,2304]{1,0:T(4,128)S(1)}, f32[80,4,2304]{2,1,0:T(4,128)S(1)}) fusion(f32[80,4,2304]{2,1,0:T(4,128)S(1)} %copy-done, f32[80,4,2304]{2,1,0:T(4,128)} %reshape.387), kind=kLoop, calls=%fused_computation.210 | loop fusion | flops 1465344 | bytes 8884224 | tf_op jit(solution)/shard_map/reduce_sum | solution.py:135
  246.1 0.9 copy-done.2
  247.0 0.6 fusion.11
  247.7 0.6 fusion.10
  248.5 0.6 fusion.9
  249.1 0.6 fusion.8
  249.8 0.7 copy-done.15
  250.5 0.6 fusion.54
  251.1 0.6 convolution_add_fusion.2
  251.7 0.6 convolution_add_fusion.1
  252.3 2.2 convolution_add_fusion
  254.5 4.7 %reshape.393 = f32[80,4,2304]{2,1,0:T(4,128)} reshape(f32[80,9216]{1,0:T(8,128)} %convolution_add_fusion) | data formatting | bytes 5898240 | tf_op jit(solution)/shard_map/reshape | solution.py:151
  259.1 4.2 %add.241 = f32[80,4,2304]{2,1,0:T(4,128)} add(f32[80,4,2304]{2,1,0:T(4,128)S(1)} %copy-done.3, f32[80,4,2304]{2,1,0:T(4,128)} %reshape.393) | non-fusion elementwise | flops 737280 | bytes 8847360 | tf_op jit(solution)/shard_map/add | solution.py:151
  (102 shorter events, 5.6 us)
Async XLA Ops:
  9.8 7.1 %copy-start.19 = (s32[2,256]{1,0:T(2,128)S(1)}, s32[2,256]{1,0:T(2,128)}, u32[]{:S(2)}) copy-start(s32[2,256]{1,0:T(2,128)} %param.12) | copy-start | bytes 6148
  9.8 7.1 %copy-start.13 = (bf16[2,32,2304]{2,1,0:T(8,128)(2,1)S(1)}, bf16[2,32,2304]{2,1,0:T(8,128)(2,1)}, u32[]{:S(2)}) copy-start(bf16[2,32,2304]{2,1,0:T(8,128)(2,1)} %param.16) | copy-start | bytes 884740
  9.8 7.8 %copy-start = (f32[80,4,2304]{2,1,0:T(4,128)S(1)}, f32[80,4,2304]{2,1,0:T(4,128)}, u32[]{:S(2)}) copy-start(f32[80,4,2304]{2,1,0:T(4,128)} %param.11) | copy-start | bytes 8847364
  9.8 215.7 %all-to-all-start = ((bf16[8,2,32,2304]{3,2,1,0:T(8,128)(2,1)}), bf16[8,2,32,2304]{3,2,1,0:T(8,128)(2,1)}, u32[]{:S(2)}, u32[]{:S(2)}) async-start(bf16[8,2,32,2304]{3,2,1,0:T(8,128)(2,1)} %broadcast_in_dim.147), calls=%async_computation | async-start | bytes 4718592 | tf_op jit(solution)/shard_map/all_to_all | solution.py:15
  16.8 132.4 %all-reduce.5.cloned.1.call-start = ((), (), s32[]{:S(2)}) async-start(), calls=%async_computation.1 | async-start | bytes 2621440 | tf_op jit(solution)/shard_map/psum | solution.py:115
  21.1 15.0 %copy-start.17 = (f32[2,256,4]{1,2,0:T(4,128)S(1)}, f32[2,256,4]{1,2,0:T(4,128)}, u32[]{:S(2)}) copy-start(f32[2,256,4]{1,2,0:T(4,128)} %param.17) | copy-start | bytes 24580
  49.4 8.5 %copy-start.14 = (f32[256,80]{1,0:T(8,128)S(1)}, f32[256,80]{1,0:T(8,128)}, u32[]{:S(2)}) copy-start(f32[256,80]{1,0:T(8,128)} %gather_fusion.5) | copy-start | bytes 245764
  49.4 10.0 %copy-start.25 = (pred[256]{0:T(512)(128)(4,1)S(1)}, pred[256]{0:T(512)(128)(4,1)}, u32[]{:S(2)}) copy-start(pred[256]{0:T(512)(128)(4,1)} %get-tuple-element.36) | copy-start | bytes 772
  49.4 10.0 %copy-start.24 = (pred[256]{0:T(512)(128)(4,1)S(1)}, pred[256]{0:T(512)(128)(4,1)}, u32[]{:S(2)}) copy-start(pred[256]{0:T(512)(128)(4,1)} %get-tuple-element.31) | copy-start | bytes 772
  54.5 5.8 %copy-start.26 = (f32[2,256]{1,0:T(2,128)S(1)}, f32[2,256]{1,0:T(2,128)}, u32[]{:S(2)}) copy-start(f32[2,256]{1,0:T(2,128)} %param.15) | copy-start | bytes 6148
  54.5 5.8 %copy-start.27 = (f32[2,256]{1,0:T(2,128)S(1)}, f32[2,256]{1,0:T(2,128)}, u32[]{:S(2)}) copy-start(f32[2,256]{1,0:T(2,128)} %param.14) | copy-start | bytes 6148
  54.5 5.8 %copy-start.28 = (f32[2,256]{1,0:T(2,128)S(1)}, f32[2,256]{1,0:T(2,128)}, u32[]{:S(2)}) copy-start(f32[2,256]{1,0:T(2,128)} %param.13) | copy-start | bytes 6148
  59.4 0.7 copy-start.12
  59.5 0.7 copy-start.11
  60.3 155.8 %all-reduce.7.cloned.1.call-start = ((), (), s32[]{:S(2)}) async-start(), calls=%async_computation.2 | async-start | bytes 2621440 | tf_op jit(solution)/shard_map/psum | solution.py:116
  60.4 0.7 copy-start.18
  216.1 6.1 %copy-start.10 = (f32[256,256]{1,0:T(8,128)S(1)}, f32[256,256]{1,0:T(8,128)}, u32[]{:S(2)}) copy-start(f32[256,256]{1,0:T(8,128)} %get-tuple-element.23) | copy-start | bytes 786436
  219.8 5.7 %copy-start.6 = (bf16[256,80]{1,0:T(8,128)(2,1)}, bf16[256,80]{1,0:T(8,128)(2,1)S(1)}, u32[]{:S(2)}) copy-start(bf16[256,80]{1,0:T(8,128)(2,1)S(1)} %get-tuple-element.60) | copy-start | bytes 122884
  219.8 5.7 %copy-start.8 = (bf16[256,80]{1,0:T(8,128)(2,1)}, bf16[256,80]{1,0:T(8,128)(2,1)S(1)}, u32[]{:S(2)}) copy-start(bf16[256,80]{1,0:T(8,128)(2,1)S(1)} %get-tuple-element.61) | copy-start | bytes 122884
  228.1 1.4 copy-start.1
  228.1 1.4 copy-start.9
  228.1 1.4 copy-start.23
  230.0 0.8 copy-start.7
  230.9 0.7 copy-start.22
  232.2 0.7 copy-start.21
  233.4 0.7 copy-start.20
  242.6 2.9 %copy-start.4 = (bf16[1,2,32,2304]{3,2,0,1:T(8,128)(2,1)S(1)}, bf16[1,2,32,2304]{3,2,0,1:T(8,128)(2,1)}, u32[]{:S(2)}) copy-start(bf16[1,2,32,2304]{3,2,0,1:T(8,128)(2,1)} %get-tuple-element.52) | copy-start | bytes 884740
  242.6 2.9 %copy-start.5 = (bf16[1,2,32,2304]{3,2,0,1:T(8,128)(2,1)S(1)}, bf16[1,2,32,2304]{3,2,0,1:T(8,128)(2,1)}, u32[]{:S(2)}) copy-start(bf16[1,2,32,2304]{3,2,0,1:T(8,128)(2,1)} %get-tuple-element.53) | copy-start | bytes 884740
  245.4 1.6 copy-start.2
  245.6 1.4 copy-start.16
  249.7 0.8 copy-start.15
  254.5 4.7 %copy-start.3 = (f32[80,4,2304]{2,1,0:T(4,128)S(1)}, f32[80,4,2304]{2,1,0:T(4,128)}, u32[]{:S(2)}) copy-start(f32[80,4,2304]{2,1,0:T(4,128)} %copy-done.2) | copy-start | bytes 8847364
Sparse Core Ops, SparseCore 0:
  60.4 88.8 all-reduce.4
  152.2 63.8 all-reduce.6
